TPU v7x, 32 devices: a whole 2x2x4 slice. The times are simulated.
32 devices in a mesh: kpt: 2 (over x), grid: 16 (over z, y, core).
Axes of the slice: x: 2, y: 2, z: 4, core: 2. Of those that a mesh axis runs over, the one named last changes fastest.
Arguments:
- orbitals: bfloat16 [4, 2, 2, 512, 256, 256], P('kpt', None, None, 'grid'), may hold values from -6 to 6
- kweights: int32 [4], P('kpt'), may hold values from 1 to 16
- occupations: int32 [4, 2], P('kpt'), may hold values from 0 to 2
- z_basis: float32 [512, 512], replicated, may hold values from -0.25 to 0.25
- z_eigen: float32 [512], replicated, may hold values from 0.25 to 4
Outputs:
- potential: float32 [512, 256, 256], P('grid')
All inputs are finite; a program needn't handle non-finite values.
Results may differ from a plain program's by a relative error of at most 0.0003.
Values sent between devices are 32-bit elements; how exact they have to be, the bound alone decides.
A program may use at most 128 MiB of HBM per device.

v0:
```python
from functools import partial

import jax
import jax.numpy as jnp
from jax import lax
from jax.sharding import PartitionSpec as P

precise = lax.Precision.HIGHEST


def real_basis(length):
    position = jnp.arange(length, dtype=jnp.int32)
    product = position[:, None] * position[None, :] % length
    angles = product.astype(jnp.float32) * (2.0 * jnp.pi / length)
    lower = position[:, None] <= length // 2
    table = jnp.where(lower, jnp.cos(angles), jnp.sin(angles))
    edges = (position == 0) | (position == length // 2)
    weights = jnp.where(edges, 1.0, 2.0).astype(jnp.float32) / length
    return (table, table * weights[:, None])


def forward_real(density, bases):
    table_x, scaled_x, table_y, scaled_y = bases
    along = jnp.einsum("zxy,ky->zxk", density, table_y, precision=precise)
    return jnp.einsum("jx,zxk->zjk", table_x, along, precision=precise)[None]


def inverse_real(planes, bases):
    table_x, scaled_x, table_y, scaled_y = bases
    half_done = jnp.einsum("jx,zjk->zxk", scaled_x, planes[0], precision=precise)
    return jnp.einsum("zxk,ky->zxy", half_done, scaled_y, precision=precise)


def scale_table(z_eigen, kx_start, kx_count, x_length, y_length):
    wave_x = (kx_start + jnp.arange(kx_count, dtype=jnp.int32)).astype(jnp.float32)
    wave_y = jnp.arange(y_length, dtype=jnp.int32).astype(jnp.float32)
    shift_x = 2.0 * jnp.sin(jnp.pi * wave_x / x_length)
    shift_y = 2.0 * jnp.sin(jnp.pi * wave_y / y_length)
    shifted = shift_x[:, None] ** 2 + shift_y[None, :] ** 2
    return 1.0 / (z_eigen[:, None, None] + shifted[None])


def kernel_columns(z_rows, factors, columns):
    projected = jnp.einsum("zj,czab->cjab", z_rows, columns, precision=precise)
    return jnp.einsum("zj,cjab->czab", z_rows, projected * factors[None], precision=precise)


def on_device(orbitals, kweights, occupations, z_basis, z_eigen):
    points = orbitals.shape[0]
    band_count = orbitals.shape[1]
    x_length = orbitals.shape[4]
    y_length = orbitals.shape[5]
    factor = (kweights[:, None] * occupations).astype(jnp.float32) / (16.0 * points * band_count)
    values = orbitals.astype(jnp.float32)
    partial_sum = jnp.sum(factor[:, :, None, None, None, None] * values * values, axis=(0, 1, 2))
    table_x, scaled_x = real_basis(x_length)
    table_y, scaled_y = real_basis(y_length)
    forward = partial(forward_real, bases=(table_x, scaled_x, table_y, scaled_y))
    inverse = partial(inverse_real, bases=(table_x, scaled_x, table_y, scaled_y))
    blocks = lax.axis_size("grid")
    density = lax.psum(partial_sum, "kpt")
    spectrum = forward(density)
    kx_count = x_length // blocks
    kx_start = lax.axis_index("grid") * kx_count
    factors = scale_table(z_eigen, kx_start, kx_count, x_length, y_length)
    columns = kernel_columns(
        z_basis, factors, lax.all_to_all(spectrum, "grid", split_axis=2, concat_axis=1, tiled=True)
    )
    planes = lax.all_to_all(columns, "grid", split_axis=1, concat_axis=2, tiled=True)
    potential = inverse(planes)
    return potential


def solution(mesh):
    return jax.shard_map(
        on_device,
        mesh=mesh,
        in_specs=(P("kpt", None, None, "grid", None, None), P("kpt"), P("kpt", None), P(), P()),
        out_specs=P("grid", None, None),
        check_vma=False,
    )
```

profile of v0, /device:TPU:13, one launch (start us, length us, event | category | flops | bytes accessed | tf_op | source)
XLA Modules:
  0.0 750.4 jit_solution(17960610065291599581)
XLA Ops:
  6.5 0.0 copy-start
  6.5 0.0 all-reduce.2.cloned.1.call-start
  6.5 0.8 convert_multiply_fusion
  7.4 18.9 %fusion = f32[32,256,256]{2,1,0:T(8,128)} fusion(bf16[2,2,2,32,256,256]{5,4,3,2,1,0:T(8,128)(2,1)} %param.5, f32[2,2]{1,0:T(2,128)S(1)} %convert_multiply_fusion), kind=kLoop, calls=%fused_computation.1 | loop fusion | flops 65011712 | bytes 41943056 | tf_op jit(solution)/shard_map/reduce_sum | solution.py:55
  26.3 0.0 all-reduce.2.cloned.1.call-update
  26.4 199.1 %all-reduce.2.cloned.1.call-done = f32[32,256,256]{2,1,0:T(8,128)} async-done(((f32[32,256,256]{2,1,0:T(8,128)}), f32[32,256,256]{2,1,0:T(8,128)}) %all-reduce.2.cloned.1.call-update) | async-done | bytes 8388624 | tf_op jit(solution)/shard_map/psum | solution.py:61
  225.5 12.7 %fusion.25 = f32[32,256,256]{1,2,0:T(8,128)S(1)} fusion(f32[32,256,256]{2,1,0:T(8,128)} %all-reduce.2.cloned.1.call-done, pred[256]{0:T(512)(128)(4,1)S(1)} %iota_compare_fusion), kind=kOutput, calls=%fused_computation.28 | convolution fusion | flops 6443433984 | bytes 16777472 | tf_op jit(solution)/shard_map/zxy,ky->zxk/dot_general | solution.py:24
  238.2 23.2 %convolution_bitcast_fusion = f32[1,32,256,256]{2,3,1,0:T(8,128)} fusion(f32[32,256,256]{1,2,0:T(8,128)S(1)} %fusion.25, pred[256]{0:T(512)(128)(4,1)S(1)} %iota_compare_fusion), kind=kOutput, calls=%fused_computation.14 | convolution fusion | flops 6443433984 | bytes 16777472 | tf_op jit(solution)/shard_map/jx,zxk->zjk/dot_general | solution.py:25
  261.4 10.3 %copy.13 = f32[1,32,256,256]{3,1,0,2:T(8,128)} copy(f32[1,32,256,256]{2,3,1,0:T(8,128)} %convolution_bitcast_fusion) | data formatting | bytes 16777216 | tf_op jit(solution)/shard_map/broadcast_in_dim | solution.py:25
  271.7 6.5 all-to-all-start
  278.3 0.1 broadcast_add_fusion
  278.4 182.2 %all-to-all-done = f32[1,32,256,256]{3,1,0,2:T(8,128)} async-done(((f32[1,32,256,256]{3,1,0,2:T(8,128)}), f32[1,32,256,256]{3,1,0,2:T(8,128)}, u32[]{:S(2)}, u32[]{:S(2)}) %all-to-all-start) | async-done | bytes 8388640 | tf_op jit(solution)/shard_map/all_to_all | solution.py:67
  460.6 8.2 %copy.14 = f32[1,32,256,256]{3,2,1,0:T(8,128)S(1)} copy(f32[1,32,256,256]{3,1,0,2:T(8,128)} %all-to-all-done) | data formatting | bytes 16777216 | tf_op jit(solution)/shard_map/all_to_all | solution.py:67
  468.8 1.4 copy.15
  470.2 0.0 copy-done
  470.2 0.0 copy-start.2
  470.2 21.4 %fusion.6 = f32[16,256,512]{2,1,0:T(8,128)S(1)} fusion(f32[512,16,256]{2,1,0:T(8,128)S(1)} %bitcast.51, f32[512,512]{1,0:T(8,128)S(1)} %copy-done), kind=kOutput, calls=%fused_computation.7 | convolution fusion | flops 12884901888 | bytes 17825792 | tf_op jit(solution)/shard_map/zj,czab->cjab/dot_general | solution.py:44
  491.7 0.0 copy-done.2
  491.7 16.4 %fusion.13 = f32[1,512,16,256]{1,3,2,0:T(8,128)} fusion(f32[16,256,512]{2,1,0:T(8,128)S(1)} %fusion.6, f32[16,256]{1,0:T(8,128)S(1)} %broadcast_add_fusion, f32[512]{0:T(512)S(1)} %copy-done.2, f32[512,512]{1,0:T(8,128)S(1)} %copy-done), kind=kOutput, calls=%fused_computation.15 | convolution fusion | flops 12891193344 | bytes 17844224 | tf_op jit(solution)/shard_map/zj,cjab->czab/dot_general | solution.py:45
  508.1 10.3 %copy.17 = f32[1,512,16,256]{3,2,0,1:T(8,128)} copy(f32[1,512,16,256]{1,3,2,0:T(8,128)} %fusion.13) | data formatting | bytes 16777216 | tf_op jit(solution)/shard_map/zj,cjab->czab/transpose | solution.py:45
  518.3 5.0 all-to-all-start.1
  523.3 182.1 %all-to-all-done.1 = f32[1,512,16,256]{3,2,0,1:T(8,128)} async-done(((f32[1,512,16,256]{3,2,0,1:T(8,128)}), f32[1,512,16,256]{3,2,0,1:T(8,128)}, u32[]{:S(2)}, u32[]{:S(2)}) %all-to-all-start.1) | async-done | bytes 8388640 | tf_op jit(solution)/shard_map/all_to_all | solution.py:69
  705.5 4.4 copy.18
  709.8 0.0 copy-start.1
  709.8 15.4 %fusion.22 = f32[32,256,256]{2,1,0:T(8,128)S(1)} fusion(f32[32,256,256]{2,1,0:T(8,128)S(1)} %bitcast.52, f32[256]{0:T(256)S(1)} %fusion.34, pred[256]{0:T(512)(128)(4,1)S(1)} %iota_compare_fusion), kind=kOutput, calls=%fused_computation.25 | convolution fusion | flops 6443499520 | bytes 16778496 | tf_op jit(solution)/shard_map/jx,zjk->zxk/dot_general | solution.py:30
  725.3 17.9 %fusion.4 = f32[32,256,256]{2,1,0:T(8,128)} fusion(f32[32,256,256]{2,1,0:T(8,128)S(1)} %fusion.22, f32[256]{0:T(256)S(1)} %fusion.34, pred[256]{0:T(512)(128)(4,1)S(1)} %iota_compare_fusion), kind=kOutput, calls=%fused_computation.5 | convolution fusion | flops 6443499520 | bytes 16778496 | tf_op jit(solution)/shard_map/zxk,ky->zxy/dot_general | solution.py:31
  743.2 0.0 copy-done.1
  (4 shorter events, 0.1 us)
Async XLA Ops:
  6.5 463.7 %copy-start = (f32[512,512]{1,0:T(8,128)S(1)}, f32[512,512]{1,0:T(8,128)}, u32[]{:S(2)}) copy-start(f32[512,512]{1,0:T(8,128)} %param.8) | copy-start | bytes 3145732
  6.5 219.0 %all-reduce.2.cloned.1.call-start = ((), (), s32[]{:S(2)}) async-start(), calls=%async_computation.2 | async-start | bytes 16777216 | tf_op jit(solution)/shard_map/psum | solution.py:61
  271.7 188.9 %all-to-all-start = ((f32[1,32,256,256]{3,1,0,2:T(8,128)}), f32[1,32,256,256]{3,1,0,2:T(8,128)}, u32[]{:S(2)}, u32[]{:S(2)}) async-start(f32[1,32,256,256]{3,1,0,2:T(8,128)} %copy.13), calls=%async_computation | async-start | bytes 16777216 | tf_op jit(solution)/shard_map/all_to_all | solution.py:67
  470.2 21.4 %copy-start.2 = (f32[512]{0:T(512)S(1)}, f32[512]{0:T(512)}, u32[]{:S(2)}) copy-start(f32[512]{0:T(512)} %param.9) | copy-start | bytes 6148
  518.3 187.1 %all-to-all-start.1 = ((f32[1,512,16,256]{3,2,0,1:T(8,128)}), f32[1,512,16,256]{3,2,0,1:T(8,128)}, u32[]{:S(2)}, u32[]{:S(2)}) async-start(f32[1,512,16,256]{3,2,0,1:T(8,128)} %copy.17), calls=%async_computation.1 | async-start | bytes 16777216 | tf_op jit(solution)/shard_map/all_to_all | solution.py:69
  709.8 33.3 %copy-start.1 = (f32[512,512]{1,0:T(8,128)S(1)}, f32[512,512]{1,0:T(8,128)}, u32[]{:S(2)}) copy-start(f32[512,512]{1,0:T(8,128)} %param.8) | copy-start | bytes 3145732
Sparse Core Ops, SparseCore 0:
  26.5 198.9 all-reduce.1
where the time goes:
time: 757 us; the launch traced here: 750 us
  waiting for transfers between devices  563 us (74%)
  matrix products  107 us (14%)
  local copies, waits for them, and re-layouts  34.6 us (5%)
  other arithmetic  20 us (3%)
  between operations  13.9 us (2%)
  starting transfers between devices  11.5 us (2%)
    psum x1, waiting for transfers between devices, on_device(): density = lax.psum(partial_sum, 'kpt')  199 us
    all_to_all x1, waiting for transfers between devices, on_device(): lax.all_to_all(spectrum, 'grid', split_axis=2, concat_axis=1, tiled=True)  182 us
    all_to_all x1, waiting for transfers between devices, on_device(): lax.all_to_all(columns, 'grid', split_axis=1, concat_axis=2, tiled=True)  182 us
    dot_general x1, matrix products, forward_real(): return jnp.einsum('jx,zxk->zjk', table_x, along, precision=precise)[None]  23.2 us
    dot_general x1, matrix products, kernel_columns(): projected = jnp.einsum('zj,czab->cjab', z_rows, columns, precision=precise)  21.4 us
    reduce_sum x1, other arithmetic, on_device(): jnp.sum(factor[:, :, None, None, None, None] * values * values, axis=(0,...  18.9 us
    dot_general x1, matrix products, inverse_real(): return jnp.einsum('zxk,ky->zxy', half_done, scaled_y, precision=precise)  17.9 us
    dot_general x1, matrix products, kernel_columns(): jnp.einsum('zj,cjab->czab', z_rows, projected * factors[None], precision=...  16.4 us
  transfers between devices with their start and end apart: 3, of which 3 were waited for; matrix products, arithmetic and copies ran while one was open for 0% of the time, Pallas kernels for 0%

commit v1 on v0

v1 whole, which is shorter than its diff:
```python
import jax
import jax.numpy as jnp
from jax import lax
from jax.sharding import PartitionSpec as P


precise = lax.Precision.HIGH
CHUNKS = 4


def real_basis(length):
    position = jnp.arange(length, dtype=jnp.int32)
    product = position[:, None] * position[None, :] % length
    angles = product.astype(jnp.float32) * (2.0 * jnp.pi / length)
    lower = position[:, None] <= length // 2
    table = jnp.where(lower, jnp.cos(angles), jnp.sin(angles))
    edges = (position == 0) | (position == length // 2)
    weights = jnp.where(edges, 1.0, 2.0).astype(jnp.float32) / length
    return (table, table * weights[:, None])


def on_device(orbitals, kweights, occupations, z_basis, z_eigen):
    points, band_count, _, planes, x_length, y_length = orbitals.shape
    z_length = z_basis.shape[0]
    groups = lax.axis_size("kpt")
    blocks = lax.axis_size("grid")
    group = lax.axis_index("kpt")
    ky_count = y_length // groups
    kx_count = x_length // blocks
    step = max(planes // CHUNKS, 1)
    chunks = planes // step
    factor = (kweights[:, None] * occupations).astype(jnp.float32) / (16.0 * points * band_count)
    table_x, scaled_x = real_basis(x_length)
    table_y, scaled_y = real_basis(y_length)

    def part_of(table, shift):
        start = lax.rem(group + shift, groups) * ky_count
        return lax.dynamic_slice_in_dim(table, start, ky_count, 0)

    def shifted_by(shift):
        return [(g, (g + shift) % groups) for g in range(groups)]

    forward_y = [part_of(table_y, shift) for shift in range(groups)]
    inverse_y = [part_of(scaled_y, shift) for shift in range(groups)]
    basis = z_basis.reshape(blocks, planes, z_length)

    projected = None
    for chunk in range(chunks):
        rows = slice(chunk * step, (chunk + 1) * step)
        values = orbitals[:, :, :, rows].astype(jnp.float32)
        density = jnp.sum(factor[:, :, None, None, None, None] * values * values, axis=(0, 1, 2))
        along = jnp.einsum("zxy,ky->zxk", density, forward_y[0], precision=precise)
        for shift in range(1, groups):
            other = jnp.einsum("zxy,ky->zxk", density, forward_y[shift], precision=precise)
            arrived = lax.ppermute(other, "kpt", shifted_by(shift))
            along = along + arrived
        spectrum = jnp.einsum("jx,zxk->zjk", table_x, along, precision=precise)
        column = lax.all_to_all(
            spectrum.reshape(step, blocks, kx_count, ky_count), "grid", split_axis=1, concat_axis=0, tiled=True
        ).reshape(blocks * step, kx_count, ky_count)
        z_rows = basis[:, rows].reshape(blocks * step, z_length)
        term = jnp.einsum("zj,zab->jab", z_rows, column, precision=precise)
        projected = term if projected is None else projected + term

    wave_x = (lax.axis_index("grid") * kx_count + jnp.arange(kx_count, dtype=jnp.int32)).astype(jnp.float32)
    wave_y = (group * ky_count + jnp.arange(ky_count, dtype=jnp.int32)).astype(jnp.float32)
    shift_x = 2.0 * jnp.sin(jnp.pi * wave_x / x_length)
    shift_y = 2.0 * jnp.sin(jnp.pi * wave_y / y_length)
    shifted = shift_x[:, None] ** 2 + shift_y[None, :] ** 2
    scaled = projected * (1.0 / (z_eigen[:, None, None] + shifted[None]))

    outputs = []
    for chunk in range(chunks):
        rows = slice(chunk * step, (chunk + 1) * step)
        z_rows = basis[:, rows].reshape(blocks * step, z_length)
        filtered = jnp.einsum("zj,jab->zab", z_rows, scaled, precision=precise)
        modes = lax.all_to_all(
            filtered.reshape(blocks, step, kx_count, ky_count), "grid", split_axis=0, concat_axis=0, tiled=True
        )
        half = jnp.einsum(
            "jx,zjk->zxk",
            scaled_x,
            modes.transpose(1, 0, 2, 3).reshape(step, x_length, ky_count),
            precision=precise,
        )
        total = jnp.einsum("zxk,ky->zxy", half, inverse_y[0], precision=precise)
        for shift in range(1, groups):
            arrived = lax.ppermute(half, "kpt", shifted_by(groups - shift))
            total = total + jnp.einsum("zxk,ky->zxy", arrived, inverse_y[shift], precision=precise)
        outputs.append(total)
    return jnp.concatenate(outputs, axis=0)


def solution(mesh):
    return jax.shard_map(
        on_device,
        mesh=mesh,
        in_specs=(P("kpt", None, None, "grid", None, None), P("kpt"), P("kpt", None), P(), P()),
        out_specs=P("grid", None, None),
        check_vma=False,
    )
```

time: 757 us -> 430 us (0.57)
  the two profiles are of different devices: /device:TPU:13 before, /device:TPU:0 now
where the time goes in v1:
time: 430 us; the launch traced here: 422 us
  waiting for transfers between devices  215 us (50%)
  matrix products  91.7 us (21%)
  starting transfers between devices  64.5 us (15%)
  local copies, waits for them, and re-layouts  25.3 us (6%)
  other arithmetic  24.7 us (6%)
    ppermute x4, waiting for transfers between devices, on_device(): arrived = lax.ppermute(other, 'kpt', shifted_by(shift))  95.4 us
    ppermute x4, waiting for transfers between devices, on_device(): arrived = lax.ppermute(half, 'kpt', shifted_by(groups - shift))  59.1 us
    all_to_all x4, waiting for transfers between devices, on_device(): lax.all_to_all(filtered.reshape(blocks, step, kx_count, ky_count), 'grid'...  53.4 us
    all_to_all x4, starting transfers between devices, on_device(): lax.all_to_all(filtered.reshape(blocks, step, kx_count, ky_count), 'grid'...  27.8 us
    all_to_all x4, starting transfers between devices, on_device(): lax.all_to_all(spectrum.reshape(step, blocks, kx_count, ky_count), 'grid'...  23.9 us
    dot_general x4, matrix products, on_device(): term = jnp.einsum('zj,zab->jab', z_rows, column, precision=precise)  21.4 us
    reduce_sum x1, other arithmetic, on_device(): jnp.sum(factor[:, :, None, None, None, None] * values * values, axis=(0,...  18.8 us
    dot_general x4, matrix products, on_device(): filtered = jnp.einsum('zj,jab->zab', z_rows, scaled, precision=precise)  15.4 us
  transfers between devices with their start and end apart: 16, of which 12 were waited for; matrix products, arithmetic and copies ran while one was open for 22% of the time, Pallas kernels for 0%

profile of v1, /device:TPU:0, one launch (start us, length us, event | category | flops | bytes accessed | tf_op | source)
XLA Modules:
  0.0 422.1 jit_solution(8932137367954698659)
XLA Ops:
  1.8 18.8 %fusion.3 = (f32[8,256,256]{2,1,0:T(8,128)S(1)}, f32[8,256,256]{2,1,0:T(8,128)}, f32[8,256,256]{2,1,0:T(8,128)}, f32[8,256,256]{2,1,0:T(8,128)S(1)}) fusion(bf16[2,2,2,32,256,256]{5,4,3,2,1,0:T(8,128)(2,1)} %param.5, f32[2,2]{1,0:T(2,128)S(1)} %convert_multiply_fusion), kind=kLoop, calls=%fused_computation.7 | loop fusion | flops 65011712 | bytes 41943056 | tf_op jit(solution)/shard_map/reduce_sum | solution.py:51
  22.0 2.0 fusion.39
  24.0 3.0 collective-permute-start.2
  27.0 23.5 %collective-permute-done.2 = f32[8,256,128]{2,1,0:T(8,128)} collective-permute-done((f32[8,256,128]{2,1,0:T(8,128)}, f32[8,256,128]{2,1,0:T(8,128)}, u32[]{:S(2)}, u32[]{:S(2)}) %collective-permute-start.2) | collective-permute-done | bytes 1048608 | tf_op jit(solution)/shard_map/ppermute | solution.py:55
  50.4 2.9 convolution_add_fusion.5
  53.3 3.8 convolution_bitcast_fusion.9
  57.1 2.5 copy.67
  59.6 2.3 copy.68
  61.9 6.4 %all-to-all-start.2 = ((f32[8,16,16,128]{3,2,0,1:T(8,128)}), f32[8,16,16,128]{3,2,0,1:T(8,128)}, u32[]{:S(2)}, u32[]{:S(2)}) async-start(f32[8,16,16,128]{3,2,0,1:T(8,128)} %copy.68), calls=%async_computation.2 | async-start | bytes 2097152 | tf_op jit(solution)/shard_map/all_to_all | solution.py:58
  68.4 2.7 fusion.43
  71.1 1.6 collective-permute-start
  72.7 24.1 %collective-permute-done = f32[8,256,128]{2,1,0:T(8,128)S(1)} collective-permute-done((f32[8,256,128]{2,1,0:T(8,128)S(1)}, f32[8,256,128]{2,1,0:T(8,128)S(1)}, u32[]{:S(2)}, u32[]{:S(2)}) %collective-permute-start) | collective-permute-done | bytes 1048608 | tf_op jit(solution)/shard_map/ppermute | solution.py:55
  97.8 3.8 convolution_bitcast_fusion.11
  101.5 2.5 copy.59
  104.1 2.3 copy.60
  106.4 5.8 %all-to-all-start = ((f32[8,16,16,128]{3,2,0,1:T(8,128)}), f32[8,16,16,128]{3,2,0,1:T(8,128)}, u32[]{:S(2)}, u32[]{:S(2)}) async-start(f32[8,16,16,128]{3,2,0,1:T(8,128)} %copy.60), calls=%async_computation | async-start | bytes 2097152 | tf_op jit(solution)/shard_map/all_to_all | solution.py:58
  112.2 2.7 fusion.41
  114.9 1.6 collective-permute-start.1
  116.5 23.9 %collective-permute-done.1 = f32[8,256,128]{2,1,0:T(8,128)S(1)} collective-permute-done((f32[8,256,128]{2,1,0:T(8,128)S(1)}, f32[8,256,128]{2,1,0:T(8,128)S(1)}, u32[]{:S(2)}, u32[]{:S(2)}) %collective-permute-start.1) | collective-permute-done | bytes 1048608 | tf_op jit(solution)/shard_map/ppermute | solution.py:55
  141.4 3.7 convolution_bitcast_fusion.10
  145.2 2.5 copy.63
  147.7 2.3 copy.64
  150.0 5.8 %all-to-all-start.1 = ((f32[8,16,16,128]{3,2,0,1:T(8,128)}), f32[8,16,16,128]{3,2,0,1:T(8,128)}, u32[]{:S(2)}, u32[]{:S(2)}) async-start(f32[8,16,16,128]{3,2,0,1:T(8,128)} %copy.64), calls=%async_computation.1 | async-start | bytes 2097152 | tf_op jit(solution)/shard_map/all_to_all | solution.py:58
  156.8 1.6 collective-permute-start.3
  158.3 23.9 %collective-permute-done.3 = f32[8,256,128]{2,1,0:T(8,128)S(1)} collective-permute-done((f32[8,256,128]{2,1,0:T(8,128)S(1)}, f32[8,256,128]{2,1,0:T(8,128)S(1)}, u32[]{:S(2)}, u32[]{:S(2)}) %collective-permute-start.3) | collective-permute-done | bytes 1048608 | tf_op jit(solution)/shard_map/ppermute | solution.py:55
  183.3 2.0 convolution_bitcast_fusion.8
  186.7 5.9 %all-to-all-start.3 = ((f32[8,16,16,128]{3,2,0,1:T(8,128)}), f32[8,16,16,128]{3,2,0,1:T(8,128)S(1)}, u32[]{:S(2)}, u32[]{:S(2)}) async-start(f32[8,16,16,128]{3,2,0,1:T(8,128)} %copy.72), calls=%async_computation.3 | async-start | bytes 2097152 | tf_op jit(solution)/shard_map/all_to_all | solution.py:58
  192.8 5.0 %fusion.7 = f32[16,128,512]{2,1,0:T(8,128)} fusion(f32[128,16,128]{2,1,0:T(8,128)} %bitcast.15, f32[16,32,512]{2,1,0:T(8,128)S(1)} %bitcast.186), kind=kOutput, calls=%fused_computation.33 | convolution fusion | flops 805306368 | bytes 5505024 | tf_op jit(solution)/shard_map/zj,zab->jab/dot_general | solution.py:62
  197.9 5.1 %fusion.9 = f32[16,128,512]{2,1,0:T(8,128)} fusion(f32[128,16,128]{2,1,0:T(8,128)} %bitcast.7, f32[16,32,512]{2,1,0:T(8,128)S(1)} %bitcast.187), kind=kOutput, calls=%fused_computation.35 | convolution fusion | flops 805306368 | bytes 5505024 | tf_op jit(solution)/shard_map/zj,zab->jab/dot_general | solution.py:62
  203.0 5.1 %fusion.5 = f32[16,128,512]{2,1,0:T(8,128)} fusion(f32[128,16,128]{2,1,0:T(8,128)} %bitcast.22, f32[16,32,512]{2,1,0:T(8,128)S(1)} %bitcast.188), kind=kOutput, calls=%fused_computation.31 | convolution fusion | flops 805306368 | bytes 5505024 | tf_op jit(solution)/shard_map/zj,zab->jab/dot_general | solution.py:62
  208.1 7.5 %all-to-all-done.3 = f32[8,16,16,128]{3,2,0,1:T(8,128)S(1)} async-done(((f32[8,16,16,128]{3,2,0,1:T(8,128)}), f32[8,16,16,128]{3,2,0,1:T(8,128)S(1)}, u32[]{:S(2)}, u32[]{:S(2)}) %all-to-all-start.3) | async-done | bytes 1048608 | tf_op jit(solution)/shard_map/all_to_all | solution.py:58
  215.5 6.2 %bitcast_multiply_fusion = f32[512,16,128]{0,2,1:T(8,128)S(1)} fusion(f32[16,128,512]{2,1,0:T(8,128)} %fusion.5, f32[16,128,512]{2,1,0:T(8,128)} %fusion.9, f32[16,128,512]{2,1,0:T(8,128)} %fusion.7, f32[16,128]{1,0:T(8,128)S(1)} %broadcast_add_fusion, f32[512]{0:T(512)S(1)} %copy-done.7, f32[128,16,128]{2,1,0:T(8,128)S(1)} %bitcast.193, ...), kind=kOutput, calls=%fused_computation.9 | convolution fusion | flops 811597824 | bytes 18098176 | tf_op jit(solution)/shard_map/zj,zab->jab/dot_general | solution.py:62
  221.7 2.2 convolution_bitcast_fusion.1
  223.9 1.6 copy.87
  225.5 7.2 %all-to-all-start.6 = ((f32[16,8,16,128]{3,2,1,0:T(8,128)}), f32[16,8,16,128]{3,2,1,0:T(8,128)S(1)}, u32[]{:S(2)}, u32[]{:S(2)}) async-start(f32[16,8,16,128]{3,2,1,0:T(8,128)} %copy.87), calls=%async_computation.6 | async-start | bytes 2097152 | tf_op jit(solution)/shard_map/all_to_all | solution.py:77
  232.7 4.4 %convolution_bitcast_fusion.2 = f32[16,8,16,128]{3,1,0,2:T(8,128)S(1)} fusion(f32[512,16,128]{0,2,1:T(8,128)} %copy-done, f32[16,32,512]{2,1,0:T(8,128)S(1)} %bitcast.191), kind=kOutput, calls=%fused_computation.16 | convolution fusion | flops 805306368 | bytes 5505024 | tf_op jit(solution)/shard_map/zj,jab->zab/dot_general | solution.py:76
  237.1 1.6 copy.81
  238.7 16.9 %all-to-all-done.6 = f32[16,8,16,128]{3,2,1,0:T(8,128)S(1)} async-done(((f32[16,8,16,128]{3,2,1,0:T(8,128)}), f32[16,8,16,128]{3,2,1,0:T(8,128)S(1)}, u32[]{:S(2)}, u32[]{:S(2)}) %all-to-all-start.6) | async-done | bytes 1048608 | tf_op jit(solution)/shard_map/all_to_all | solution.py:77
  255.6 6.8 %all-to-all-start.5 = ((f32[16,8,16,128]{3,2,1,0:T(8,128)}), f32[16,8,16,128]{3,2,1,0:T(8,128)S(1)}, u32[]{:S(2)}, u32[]{:S(2)}) async-start(f32[16,8,16,128]{3,2,1,0:T(8,128)} %copy.81), calls=%async_computation.5 | async-start | bytes 2097152 | tf_op jit(solution)/shard_map/all_to_all | solution.py:77
  262.4 4.4 %convolution_bitcast_fusion.3 = f32[16,8,16,128]{3,1,0,2:T(8,128)S(1)} fusion(f32[512,16,128]{0,2,1:T(8,128)} %copy-done, f32[16,32,512]{2,1,0:T(8,128)S(1)} %bitcast.192), kind=kOutput, calls=%fused_computation.17 | convolution fusion | flops 805306368 | bytes 5505024 | tf_op jit(solution)/shard_map/zj,jab->zab/dot_general | solution.py:76
  266.8 1.6 copy.75
  268.4 16.9 %all-to-all-done.5 = f32[16,8,16,128]{3,2,1,0:T(8,128)S(1)} async-done(((f32[16,8,16,128]{3,2,1,0:T(8,128)}), f32[16,8,16,128]{3,2,1,0:T(8,128)S(1)}, u32[]{:S(2)}, u32[]{:S(2)}) %all-to-all-start.5) | async-done | bytes 1048608 | tf_op jit(solution)/shard_map/all_to_all | solution.py:77
  285.3 6.8 %all-to-all-start.4 = ((f32[16,8,16,128]{3,2,1,0:T(8,128)}), f32[16,8,16,128]{3,2,1,0:T(8,128)S(1)}, u32[]{:S(2)}, u32[]{:S(2)}) async-start(f32[16,8,16,128]{3,2,1,0:T(8,128)} %copy.75), calls=%async_computation.4 | async-start | bytes 2097152 | tf_op jit(solution)/shard_map/all_to_all | solution.py:77
  292.1 4.4 %convolution_bitcast_fusion = f32[16,8,16,128]{3,1,0,2:T(8,128)S(1)} fusion(f32[512,16,128]{0,2,1:T(8,128)} %copy-done, f32[16,32,512]{2,1,0:T(8,128)} %bitcast.185), kind=kOutput, calls=%fused_computation.14 | convolution fusion | flops 805306368 | bytes 5505024 | tf_op jit(solution)/shard_map/zj,jab->zab/dot_general | solution.py:76
  296.5 1.6 copy.93
  298.1 16.9 %all-to-all-done.4 = f32[16,8,16,128]{3,2,1,0:T(8,128)S(1)} async-done(((f32[16,8,16,128]{3,2,1,0:T(8,128)}), f32[16,8,16,128]{3,2,1,0:T(8,128)S(1)}, u32[]{:S(2)}, u32[]{:S(2)}) %all-to-all-start.4) | async-done | bytes 1048608 | tf_op jit(solution)/shard_map/all_to_all | solution.py:77
  315.0 7.0 %all-to-all-start.7 = ((f32[16,8,16,128]{3,2,1,0:T(8,128)}), f32[16,8,16,128]{3,2,1,0:T(8,128)}, u32[]{:S(2)}, u32[]{:S(2)}) async-start(f32[16,8,16,128]{3,2,1,0:T(8,128)} %copy.93), calls=%async_computation.7 | async-start | bytes 2097152 | tf_op jit(solution)/shard_map/all_to_all | solution.py:77
  322.1 2.0 convolution_bitcast_fusion.7
  324.1 1.6 collective-permute-start.4
  325.7 3.0 convolution_bitcast_fusion.6
  329.3 3.0 convolution_bitcast_fusion.5
  333.8 2.4 fusion.35
  336.2 3.6 fusion.33
  339.7 2.2 fusion.31
  342.0 2.8 all-to-all-done.7
  346.1 2.0 convolution_bitcast_fusion.4
  348.1 1.6 collective-permute-start.7
  350.9 2.4 convolution_add_fusion.3
  353.3 19.4 %collective-permute-done.5 = f32[8,256,128]{1,2,0:T(8,128)} collective-permute-done((f32[8,256,128]{1,2,0:T(8,128)}, f32[8,256,128]{1,2,0:T(8,128)}, u32[]{:S(2)}, u32[]{:S(2)}) %collective-permute-start.5) | collective-permute-done | bytes 1048608 | tf_op jit(solution)/shard_map/ppermute | solution.py:88
  372.7 2.2 convolution_add_fusion.2
  375.0 20.2 %collective-permute-done.6 = f32[8,256,128]{1,2,0:T(8,128)} collective-permute-done((f32[8,256,128]{1,2,0:T(8,128)}, f32[8,256,128]{1,2,0:T(8,128)}, u32[]{:S(2)}, u32[]{:S(2)}) %collective-permute-start.6) | collective-permute-done | bytes 1048608 | tf_op jit(solution)/shard_map/ppermute | solution.py:88
  395.2 2.2 convolution_add_fusion.1
  397.5 19.5 %collective-permute-done.7 = f32[8,256,128]{1,2,0:T(8,128)S(1)} collective-permute-done((f32[8,256,128]{1,2,0:T(8,128)S(1)}, f32[8,256,128]{1,2,0:T(8,128)S(1)}, u32[]{:S(2)}, u32[]{:S(2)}) %collective-permute-start.7) | collective-permute-done | bytes 1048608 | tf_op jit(solution)/shard_map/ppermute | solution.py:88
  418.0 3.9 pad_maximum_fusion
  (41 shorter events, 14.7 us)
Async XLA Ops:
  20.7 1.3 copy-start.3
  24.0 26.5 %collective-permute-start.2 = (f32[8,256,128]{2,1,0:T(8,128)}, f32[8,256,128]{2,1,0:T(8,128)}, u32[]{:S(2)}, u32[]{:S(2)}) collective-permute-start(f32[8,256,128]{2,1,0:T(8,128)} %fusion.39), channel_id=1, source_target_pairs={{0,16},{16,0},{1,17},{17,1},{2,18},{18,2},{3,19},{19,3},{4,20},{20... | collective-permute-start | bytes 3145736 | tf_op jit(solution)/shard_map/ppermute | solution.py:55
  61.9 44.5 %all-to-all-start.2 = ((f32[8,16,16,128]{3,2,0,1:T(8,128)}), f32[8,16,16,128]{3,2,0,1:T(8,128)}, u32[]{:S(2)}, u32[]{:S(2)}) async-start(f32[8,16,16,128]{3,2,0,1:T(8,128)} %copy.68), calls=%async_computation.2 | async-start | bytes 2097152 | tf_op jit(solution)/shard_map/all_to_all | solution.py:58
  68.4 28.4 %copy-start.2 = (f32[8,256,256]{2,1,0:T(8,128)S(1)}, f32[8,256,256]{2,1,0:T(8,128)}, u32[]{:S(2)}) copy-start(f32[8,256,256]{2,1,0:T(8,128)} %get-tuple-element.7) | copy-start | bytes 6291460
  71.1 25.6 %collective-permute-start = (f32[8,256,128]{2,1,0:T(8,128)S(1)}, f32[8,256,128]{2,1,0:T(8,128)S(1)}, u32[]{:S(2)}, u32[]{:S(2)}) collective-permute-start(f32[8,256,128]{2,1,0:T(8,128)S(1)} %fusion.43), channel_id=1, source_target_pairs={{0,16},{16,0},{1,17},{17,1},{2,18},{18,2},{3,19},{19,3},{4,20},{20... | collective-permute-start | bytes 3145736 | tf_op jit(solution)/shard_map/ppermute | solution.py:55
  106.4 43.6 %all-to-all-start = ((f32[8,16,16,128]{3,2,0,1:T(8,128)}), f32[8,16,16,128]{3,2,0,1:T(8,128)}, u32[]{:S(2)}, u32[]{:S(2)}) async-start(f32[8,16,16,128]{3,2,0,1:T(8,128)} %copy.60), calls=%async_computation | async-start | bytes 2097152 | tf_op jit(solution)/shard_map/all_to_all | solution.py:58
  112.2 28.2 %copy-start.1 = (f32[8,256,256]{2,1,0:T(8,128)S(1)}, f32[8,256,256]{2,1,0:T(8,128)}, u32[]{:S(2)}) copy-start(f32[8,256,256]{2,1,0:T(8,128)} %get-tuple-element.6) | copy-start | bytes 6291460
  114.9 25.5 %collective-permute-start.1 = (f32[8,256,128]{2,1,0:T(8,128)S(1)}, f32[8,256,128]{2,1,0:T(8,128)S(1)}, u32[]{:S(2)}, u32[]{:S(2)}) collective-permute-start(f32[8,256,128]{2,1,0:T(8,128)S(1)} %fusion.41), channel_id=1, source_target_pairs={{0,16},{16,0},{1,17},{17,1},{2,18},{18,2},{3,19},{19,3},{4,20},{20... | collective-permute-start | bytes 3145736 | tf_op jit(solution)/shard_map/ppermute | solution.py:55
  150.0 36.7 %all-to-all-start.1 = ((f32[8,16,16,128]{3,2,0,1:T(8,128)}), f32[8,16,16,128]{3,2,0,1:T(8,128)}, u32[]{:S(2)}, u32[]{:S(2)}) async-start(f32[8,16,16,128]{3,2,0,1:T(8,128)} %copy.64), calls=%async_computation.1 | async-start | bytes 2097152 | tf_op jit(solution)/shard_map/all_to_all | solution.py:58
  156.8 25.5 %collective-permute-start.3 = (f32[8,256,128]{2,1,0:T(8,128)S(1)}, f32[8,256,128]{2,1,0:T(8,128)S(1)}, u32[]{:S(2)}, u32[]{:S(2)}) collective-permute-start(f32[8,256,128]{2,1,0:T(8,128)S(1)} %fusion.37), channel_id=1, source_target_pairs={{0,16},{16,0},{1,17},{17,1},{2,18},{18,2},{3,19},{19,3},{4,20},{20... | collective-permute-start | bytes 3145736 | tf_op jit(solution)/shard_map/ppermute | solution.py:55
  185.6 7.2 %copy-start.6 = (f32[512,512]{1,0:T(8,128)S(1)}, f32[512,512]{1,0:T(8,128)}, u32[]{:S(2)}) copy-start(f32[512,512]{1,0:T(8,128)} %param.8) | copy-start | bytes 3145732
  186.7 28.8 %all-to-all-start.3 = ((f32[8,16,16,128]{3,2,0,1:T(8,128)}), f32[8,16,16,128]{3,2,0,1:T(8,128)S(1)}, u32[]{:S(2)}, u32[]{:S(2)}) async-start(f32[8,16,16,128]{3,2,0,1:T(8,128)} %copy.72), calls=%async_computation.3 | async-start | bytes 2097152 | tf_op jit(solution)/shard_map/all_to_all | solution.py:58
  203.0 12.6 %copy-start.7 = (f32[512]{0:T(512)S(1)}, f32[512]{0:T(512)}, u32[]{:S(2)}) copy-start(f32[512]{0:T(512)} %param.9) | copy-start | bytes 6148
  221.7 2.2 copy-start
  225.5 30.1 %all-to-all-start.6 = ((f32[16,8,16,128]{3,2,1,0:T(8,128)}), f32[16,8,16,128]{3,2,1,0:T(8,128)S(1)}, u32[]{:S(2)}, u32[]{:S(2)}) async-start(f32[16,8,16,128]{3,2,1,0:T(8,128)} %copy.87), calls=%async_computation.6 | async-start | bytes 2097152 | tf_op jit(solution)/shard_map/all_to_all | solution.py:77
  255.6 29.7 %all-to-all-start.5 = ((f32[16,8,16,128]{3,2,1,0:T(8,128)}), f32[16,8,16,128]{3,2,1,0:T(8,128)S(1)}, u32[]{:S(2)}, u32[]{:S(2)}) async-start(f32[16,8,16,128]{3,2,1,0:T(8,128)} %copy.81), calls=%async_computation.5 | async-start | bytes 2097152 | tf_op jit(solution)/shard_map/all_to_all | solution.py:77
  285.3 29.7 %all-to-all-start.4 = ((f32[16,8,16,128]{3,2,1,0:T(8,128)}), f32[16,8,16,128]{3,2,1,0:T(8,128)S(1)}, u32[]{:S(2)}, u32[]{:S(2)}) async-start(f32[16,8,16,128]{3,2,1,0:T(8,128)} %copy.75), calls=%async_computation.4 | async-start | bytes 2097152 | tf_op jit(solution)/shard_map/all_to_all | solution.py:77
  315.0 29.8 %all-to-all-start.7 = ((f32[16,8,16,128]{3,2,1,0:T(8,128)}), f32[16,8,16,128]{3,2,1,0:T(8,128)}, u32[]{:S(2)}, u32[]{:S(2)}) async-start(f32[16,8,16,128]{3,2,1,0:T(8,128)} %copy.93), calls=%async_computation.7 | async-start | bytes 2097152 | tf_op jit(solution)/shard_map/all_to_all | solution.py:77
  324.1 26.8 %collective-permute-start.4 = (f32[8,256,128]{1,2,0:T(8,128)S(1)}, f32[8,256,128]{1,2,0:T(8,128)}, u32[]{:S(2)}, u32[]{:S(2)}) collective-permute-start(f32[8,256,128]{1,2,0:T(8,128)S(1)} %convolution_bitcast_fusion.7), channel_id=1, source_target_pairs={{0,16},{16,0},{1,17},{17,1},{2,18},{18,2},{3,19},{19,3},{4,20},{20... | collective-permute-start | bytes 3145736 | tf_op jit(solution)/shard_map/ppermute | solution.py:88
  328.7 44.0 %collective-permute-start.5 = (f32[8,256,128]{1,2,0:T(8,128)}, f32[8,256,128]{1,2,0:T(8,128)}, u32[]{:S(2)}, u32[]{:S(2)}) collective-permute-start(f32[8,256,128]{1,2,0:T(8,128)} %convolution_bitcast_fusion.6), channel_id=1, source_target_pairs={{0,16},{16,0},{1,17},{17,1},{2,18},{18,2},{3,19},{19,3},{4,20},{20... | collective-permute-start | bytes 3145736 | tf_op jit(solution)/shard_map/ppermute | solution.py:88
  332.3 62.9 %collective-permute-start.6 = (f32[8,256,128]{1,2,0:T(8,128)}, f32[8,256,128]{1,2,0:T(8,128)}, u32[]{:S(2)}, u32[]{:S(2)}) collective-permute-start(f32[8,256,128]{1,2,0:T(8,128)} %convolution_bitcast_fusion.5), channel_id=1, source_target_pairs={{0,16},{16,0},{1,17},{17,1},{2,18},{18,2},{3,19},{19,3},{4,20},{20... | collective-permute-start | bytes 3145736 | tf_op jit(solution)/shard_map/ppermute | solution.py:88
  348.1 2.9 copy-start.5
  348.1 68.9 %collective-permute-start.7 = (f32[8,256,128]{1,2,0:T(8,128)S(1)}, f32[8,256,128]{1,2,0:T(8,128)S(1)}, u32[]{:S(2)}, u32[]{:S(2)}) collective-permute-start(f32[8,256,128]{1,2,0:T(8,128)S(1)} %convolution_bitcast_fusion.4), channel_id=1, source_target_pairs={{0,16},{16,0},{1,17},{17,1},{2,18},{18,2},{3,19},{19,3},{4,20},{20... | collective-permute-start | bytes 3145736 | tf_op jit(solution)/shard_map/ppermute | solution.py:88
  350.9 21.8 %copy-start.4 = (f32[8,256,256]{2,1,0:T(8,128)S(1)}, f32[8,256,256]{2,1,0:T(8,128)}, u32[]{:S(2)}) copy-start(f32[8,256,256]{2,1,0:T(8,128)} %fusion.33) | copy-start | bytes 6291460
